TPU v7x, 512 devices: a whole 4x8x8 slice. The times are simulated.
512 devices in a mesh: gx: 4 (over y_lo), gy: 16 (over y_hi, z), gz: 8 (over x, core).
Axes of the slice: x: 4, y: 8 (y_hi: 2, y_lo: 4; y = y_hi * 4 + y_lo), z: 8, core: 2. Of those that a mesh axis runs over, the one named last changes fastest.
Arguments:
- grads: float32 [4, 16, 8, 160, 4096], P('gx', 'gy', 'gz'), may hold values from -6 to 6
- peer_table: int32 [16], replicated, may hold values from 0 to 15, each once
- layer_offsets: int32 [2], replicated, may hold values from 0 to 96, as said below
Outputs:
- averaged: float32 [4, 16, 8, 128, 4096], P('gx', 'gy', 'gz')
Inputs may be any that keep to these rules, and one draw needn't show every extreme that they name: layer_offsets[l] is a multiple of 8 between l * (80) and l * 80 + 16; the last layer's offset is the largest of these.
All inputs are finite; a program needn't handle non-finite values.
Results may differ from a plain program's by a relative error of at most 0.00002.
Values sent between devices are 32-bit elements; how exact they have to be, the bound alone decides.
No kernel may reach another device: no remote copies, remote signals or barrier semaphores. Data moves between devices by JAX's collectives and lax.ppermute only.
A program may use at most 64 MiB of HBM per device.

v0:
```python
import jax
import jax.numpy as jnp
from jax import lax
from jax.sharding import PartitionSpec as P

ROWS = 64
LAYERS = 2


def filled_up(lines, peers):
    spare = -lines.shape[0] % peers
    if not spare:
        return lines
    return jnp.concatenate([lines, jnp.zeros((spare, *lines.shape[1:]), lines.dtype)])


def sum_by_parts(shard, axis):
    lines = shard.reshape(-1, *shard.shape[1:][-1:])
    own = lax.psum_scatter(
        filled_up(lines, lax.axis_size(axis)), axis, scatter_dimension=0, tiled=True
    )
    whole = lax.all_gather(own, axis).reshape(-1, *lines.shape[1:])
    return lax.slice_in_dim(whole, 0, len(lines)).reshape(shard.shape)


def on_device(grads, peer_table, layer_offsets):
    buffer = grads[0, 0, 0]
    pieces = [lax.dynamic_slice_in_dim(buffer, layer_offsets[i], ROWS, 0) for i in range(LAYERS)]
    packed = jnp.concatenate(pieces, axis=0)
    count_y = lax.axis_size("gy")
    group_b = min(8, count_y)
    group_a = lax.axis_size("gx") * (count_y // group_b)
    places = jnp.arange(count_y, dtype=jnp.int32)
    onehot = (peer_table[:, None] == places[None, :]).astype(jnp.int32)
    inverse = jnp.sum(onehot * places[:, None], axis=0)
    spread = lax.all_to_all(packed[None], "gy", split_axis=1, concat_axis=0, tiled=True)
    current = jnp.take(spread, peer_table, axis=0)
    total_c = sum_by_parts(current, "gz")
    current = 0.5 * current + 0.5 / lax.axis_size("gz") * total_c
    block_rows = current.shape[1]
    width = current.shape[2]
    split = current.reshape(count_y // group_b, group_b, block_rows, width)
    total_b = jnp.sum(split, axis=1, keepdims=True)
    split = 0.5 * split + 0.5 / group_b * total_b
    local_a = jnp.sum(split, axis=0, keepdims=True)
    total_a = lax.psum(local_a, "gx")
    split = 0.5 * split + 0.5 / group_a * total_a
    current = jnp.take(split.reshape(count_y, block_rows, width), inverse, axis=0)
    result = lax.all_to_all(current, "gy", split_axis=0, concat_axis=1, tiled=True)[0]
    return result[None, None, None]


def solution(mesh):
    placed = (P("gx", "gy", "gz", None, None), P(), P())
    return jax.shard_map(
        on_device,
        mesh=mesh,
        in_specs=placed,
        out_specs=P("gx", "gy", "gz", None, None),
        check_vma=False,
    )
```

profile of v0, /device:TPU:8, one launch (start us, length us, event | category | flops | bytes accessed | tf_op | source)
XLA Modules:
  0.0 328.4 jit_solution(8673940467536958085)
XLA Ops:
  6.5 1.4 fusion.2
  11.8 1.8 dynamic-slice_bitcast_fusion.1
  13.6 0.1 pad_maximum_fusion
  13.7 3.7 %broadcast_in_dim.19 = f32[1,128,4096]{2,0,1:T(1,128)} reshape(f32[128,4096]{1,0:T(8,128)S(1)} %pad_maximum_fusion) | data formatting | bytes 4194304 | tf_op jit(solution)/shard_map/broadcast_in_dim | solution.py:36
  17.4 0.0 copy-start.2
  17.4 14.9 %all-to-all-start = ((f32[1,128,4096]{2,0,1:T(1,128)}), f32[1,128,4096]{2,0,1:T(1,128)S(1)}, u32[]{:S(2)}, u32[]{:S(2)}) async-start(f32[1,128,4096]{2,0,1:T(1,128)} %broadcast_in_dim.19), calls=%async_computation | async-start | bytes 4194304 | tf_op jit(solution)/shard_map/all_to_all | solution.py:36
  32.4 0.0 reduce-scatter.2.cloned.1.call-start
  32.4 0.0 copy-done.2
  32.5 57.0 %all-to-all-done = f32[1,128,4096]{2,0,1:T(1,128)S(1)} async-done(((f32[1,128,4096]{2,0,1:T(1,128)}), f32[1,128,4096]{2,0,1:T(1,128)S(1)}, u32[]{:S(2)}, u32[]{:S(2)}) %all-to-all-start) | async-done | bytes 2097184 | tf_op jit(solution)/shard_map/all_to_all | solution.py:36
  89.5 3.0 copy.6
  92.4 2.3 gather_fusion
  94.7 1.6 select_bitcast_fusion
  96.3 0.0 reduce-scatter.2.cloned.1.call-update
  96.3 0.0 all-gather.3.cloned.1.call-start
  96.4 48.3 %reduce-scatter.2.cloned.1.call-done = f32[16,4096]{1,0:T(8,128)} async-done(((f32[128,4096]{1,0:T(8,128)}), f32[16,4096]{1,0:T(8,128)}) %reduce-scatter.2.cloned.1.call-update) | async-done | bytes 262160 | tf_op jit(solution)/shard_map/reduce_scatter | solution.py:19
  144.7 0.0 all-gather.3.cloned.1.call-update
  144.7 0.0 all-reduce.2.cloned.1.call-start
  144.7 31.6 %all-gather.3.cloned.1.call-done = f32[128,4096]{1,0:T(8,128)} async-done(((f32[16,4096]{1,0:T(8,128)}), f32[128,4096]{1,0:T(8,128)}) %all-gather.3.cloned.1.call-update) | async-done | bytes 2097168 | tf_op jit(solution)/shard_map/all_gather | solution.py:22
  176.4 2.1 bitcast_reduce_fusion
  178.5 0.0 copy-start
  178.5 1.3 copy-done
  179.8 0.2 fusion.1
  180.0 1.2 reduce_sum.28
  181.3 0.0 copy-start.1
  181.3 0.0 all-reduce.2.cloned.1.call-update
  181.3 0.1 select_reduce_fusion
  181.4 68.4 %all-reduce.2.cloned.1.call-done = f32[1,8,8,4096]{3,2,1,0:T(8,128)} async-done(((f32[1,8,8,4096]{3,2,1,0:T(8,128)}), f32[1,8,8,4096]{3,2,1,0:T(8,128)}) %all-reduce.2.cloned.1.call-update) | async-done | bytes 1048592 | tf_op jit(solution)/shard_map/psum | solution.py:46
  249.8 1.3 multiply_bitcast_fusion
  251.1 0.0 copy-done.1
  251.1 1.6 bitcast_add_fusion
  252.7 2.3 gather_fusion.1
  255.0 0.3 broadcast_select_fusion
  255.2 65.4 %all_to_all.21 = f32[16,8,4096]{2,1,0:T(8,128)S(1)} all-to-all(f32[16,8,4096]{2,1,0:T(8,128)S(1)} %broadcast_select_fusion), channel_id=1, replica_groups=mesh['gx'=4,'gy'=16,'gz'=8] {'gy'}, dimensions={0} | all-to-all | bytes 4194304 | tf_op jit(solution)/shard_map/all_to_all | solution.py:49
  320.6 1.3 copy.9
  (7 shorter events, 0.1 us)
Async XLA Ops:
  17.4 15.0 %copy-start.2 = (s32[16]{0:T(128)S(1)}, s32[16]{0:T(128)}, u32[]{:S(2)}) copy-start(s32[16]{0:T(128)} %param.6) | copy-start | bytes 196
  17.4 72.0 %all-to-all-start = ((f32[1,128,4096]{2,0,1:T(1,128)}), f32[1,128,4096]{2,0,1:T(1,128)S(1)}, u32[]{:S(2)}, u32[]{:S(2)}) async-start(f32[1,128,4096]{2,0,1:T(1,128)} %broadcast_in_dim.19), calls=%async_computation | async-start | bytes 4194304 | tf_op jit(solution)/shard_map/all_to_all | solution.py:36
  32.4 112.3 %reduce-scatter.2.cloned.1.call-start = ((), (), s32[]{:S(2)}) async-start(), calls=%async_computation.3 | async-start | bytes 2359296 | tf_op jit(solution)/shard_map/reduce_scatter | solution.py:19
  96.3 80.1 %all-gather.3.cloned.1.call-start = ((), (), s32[]{:S(2)}) async-start(), calls=%async_computation.5 | async-start | bytes 2359296 | tf_op jit(solution)/shard_map/all_gather | solution.py:22
  144.7 105.1 %all-reduce.2.cloned.1.call-start = ((), (), s32[]{:S(2)}) async-start(), calls=%async_computation.4 | async-start | bytes 2097152 | tf_op jit(solution)/shard_map/psum | solution.py:46
  178.5 1.3 copy-start
  181.3 69.8 %copy-start.1 = (f32[16,8,4096]{2,1,0:T(8,128)S(1)}, f32[16,8,4096]{2,1,0:T(8,128)}, u32[]{:S(2)}) copy-start(f32[16,8,4096]{2,1,0:T(8,128)} %copy-done) | copy-start | bytes 6291460
Sparse Core Ops, SparseCore 0:
  96.4 48.1 reduce-scatter.1
  146.8 29.5 all-gather.2
  181.4 68.3 all-reduce.1
where the time goes:
time: 329 us; the launch traced here: 328 us
  waiting for transfers between devices  205 us (62%)
  blocking collectives  65.4 us (20%)
  between operations  17.1 us (5%)
  local copies, waits for them, and re-layouts  17 us (5%)
  starting transfers between devices  15 us (5%)
  other arithmetic  8.57 us (3%)
    psum x1, waiting for transfers between devices, on_device(): total_a = lax.psum(local_a, 'gx')  68.4 us
    all_to_all x1, blocking collectives, on_device(): lax.all_to_all(current, 'gy', split_axis=0, concat_axis=1, tiled=True)[0]  65.4 us
    all_to_all x1, waiting for transfers between devices, on_device(): lax.all_to_all(packed[None], 'gy', split_axis=1, concat_axis=0, tiled=True)  57 us
    reduce_scatter x1, waiting for transfers between devices, sum_by_parts(): lax.psum_scatter(filled_up(lines, lax.axis_size(axis)), axis, scatter_dim...  48.3 us
    all_gather x1, waiting for transfers between devices, sum_by_parts(): whole = lax.all_gather(own, axis).reshape(-1, *lines.shape[1:])  31.6 us
    all_to_all x1, starting transfers between devices, on_device(): lax.all_to_all(packed[None], 'gy', split_axis=1, concat_axis=0, tiled=True)  14.9 us
  transfers between devices with their start and end apart: 4, of which 4 were waited for; matrix products, arithmetic and copies ran while one was open for 0% of the time, Pallas kernels for 0%

commit v1 on v0

--- a/solution.py
+++ b/solution.py
@@ -5,6 +5,11 @@
 
 ROWS = 64
 LAYERS = 2
+
+
+def gather_and_add(x, axis):
+    parts = lax.all_gather(x, axis)
+    return jnp.sum(parts, axis=0)
 
 
 def filled_up(lines, peers):
@@ -43,7 +48,7 @@
     total_b = jnp.sum(split, axis=1, keepdims=True)
     split = 0.5 * split + 0.5 / group_b * total_b
     local_a = jnp.sum(split, axis=0, keepdims=True)
-    total_a = lax.psum(local_a, "gx")
+    total_a = gather_and_add(local_a, "gx")
     split = 0.5 * split + 0.5 / group_a * total_a
     current = jnp.take(split.reshape(count_y, block_rows, width), inverse, axis=0)
     result = lax.all_to_all(current, "gy", split_axis=0, concat_axis=1, tiled=True)[0]

time: 329 us -> 349 us (1.061)
  the two profiles are of different devices: /device:TPU:8 before, /device:TPU:16 now
where the time goes in v1:
time: 349 us
  waiting for transfers between devices  225 us (64%)
  blocking collectives  64.3 us (18%)
  local copies, waits for them, and re-layouts  18.2 us (5%)
  between operations  17.1 us (5%)
  starting transfers between devices  14.1 us (4%)
  other arithmetic  10.1 us (3%)
    all_gather x1, waiting for transfers between devices, gather_and_add(): parts = lax.all_gather(x, axis)  87 us
    all_to_all x1, blocking collectives, on_device(): lax.all_to_all(current, 'gy', split_axis=0, concat_axis=1, tiled=True)[0]  64.3 us
    all_to_all x1, waiting for transfers between devices, on_device(): lax.all_to_all(packed[None], 'gy', split_axis=1, concat_axis=0, tiled=True)  60.1 us
    reduce_scatter x1, waiting for transfers between devices, sum_by_parts(): lax.psum_scatter(filled_up(lines, lax.axis_size(axis)), axis, scatter_dim...  46.1 us
    all_gather x1, waiting for transfers between devices, sum_by_parts(): whole = lax.all_gather(own, axis).reshape(-1, *lines.shape[1:])  31.5 us
    all_to_all x1, starting transfers between devices, on_device(): lax.all_to_all(packed[None], 'gy', split_axis=1, concat_axis=0, tiled=True)  14 us
    unnamed x8, local copies, waits for them, and re-layouts  7.06 us
  transfers between devices with their start and end apart: 4, of which 4 were waited for; matrix products, arithmetic and copies ran while one was open for 0% of the time, Pallas kernels for 0%

profile of v1, /device:TPU:16, one launch (start us, length us, event | category | flops | bytes accessed | tf_op | source)
XLA Modules:
  0.0 348.7 jit_solution(8881388975369387660)
XLA Ops:
  6.5 1.4 fusion.2
  11.8 1.8 dynamic-slice_bitcast_fusion.1
  13.6 0.1 pad_maximum_fusion
  13.7 3.7 %broadcast_in_dim.16 = f32[1,128,4096]{2,0,1:T(1,128)} reshape(f32[128,4096]{1,0:T(8,128)S(1)} %pad_maximum_fusion) | data formatting | bytes 4194304 | tf_op jit(solution)/shard_map/broadcast_in_dim | solution.py:41
  17.4 0.0 copy-start.2
  17.4 14.0 %all-to-all-start = ((f32[1,128,4096]{2,0,1:T(1,128)}), f32[1,128,4096]{2,0,1:T(1,128)S(1)}, u32[]{:S(2)}, u32[]{:S(2)}) async-start(f32[1,128,4096]{2,0,1:T(1,128)} %broadcast_in_dim.16), calls=%async_computation | async-start | bytes 4194304 | tf_op jit(solution)/shard_map/all_to_all | solution.py:41
  31.5 0.0 reduce-scatter.2.cloned.1.call-start
  31.5 0.0 copy-done.2
  31.6 60.1 %all-to-all-done = f32[1,128,4096]{2,0,1:T(1,128)S(1)} async-done(((f32[1,128,4096]{2,0,1:T(1,128)}), f32[1,128,4096]{2,0,1:T(1,128)S(1)}, u32[]{:S(2)}, u32[]{:S(2)}) %all-to-all-start) | async-done | bytes 2097184 | tf_op jit(solution)/shard_map/all_to_all | solution.py:41
  91.7 3.0 copy.6
  94.6 2.3 gather_fusion
  96.9 1.6 select_bitcast_fusion
  98.5 0.0 reduce-scatter.2.cloned.1.call-update
  98.5 0.0 all-gather.5.cloned.1.call-start
  98.6 46.1 %reduce-scatter.2.cloned.1.call-done = f32[16,4096]{1,0:T(8,128)} async-done(((f32[128,4096]{1,0:T(8,128)}), f32[16,4096]{1,0:T(8,128)}) %reduce-scatter.2.cloned.1.call-update) | async-done | bytes 262160 | tf_op jit(solution)/shard_map/reduce_scatter | solution.py:24
  144.7 0.0 all-gather.5.cloned.1.call-update
  144.7 0.0 all-gather.7.cloned.1.call-start
  144.7 31.5 %all-gather.5.cloned.1.call-done = f32[128,4096]{1,0:T(8,128)} async-done(((f32[16,4096]{1,0:T(8,128)}), f32[128,4096]{1,0:T(8,128)}) %all-gather.5.cloned.1.call-update) | async-done | bytes 2097168 | tf_op jit(solution)/shard_map/all_gather | solution.py:27
  176.3 2.1 bitcast_reduce_fusion
  178.4 0.0 copy-start
  178.4 1.3 copy-done
  179.7 0.2 fusion.1
  179.9 1.2 reduce_sum.37
  181.1 0.0 all-gather.7.cloned.1.call-update
  181.1 0.1 select_reduce_fusion
  181.3 87.0 %all-gather.7.cloned.1.call-done = f32[32,8,4096]{2,1,0:T(8,128)} async-done(((f32[8,8,4096]{2,1,0:T(8,128)}), f32[32,8,4096]{2,1,0:T(8,128)}) %all-gather.7.cloned.1.call-update) | async-done | bytes 4194320 | tf_op jit(solution)/shard_map/all_gather | solution.py:11
  268.3 2.5 reduce.1
  270.8 0.0 copy-start.1
  270.8 0.1 broadcast_multiply_fusion
  270.9 1.5 copy-done.1
  272.4 0.3 bitcast_add_fusion
  272.7 2.0 gather_fusion.1
  274.7 1.9 broadcast_select_fusion
  276.6 64.3 %all_to_all.21 = f32[16,8,4096]{2,1,0:T(8,128)S(1)} all-to-all(f32[16,8,4096]{2,1,0:T(8,128)S(1)} %broadcast_select_fusion), channel_id=1, replica_groups=mesh['gx'=4,'gy'=16,'gz'=8] {'gy'}, dimensions={0} | all-to-all | bytes 4194304 | tf_op jit(solution)/shard_map/all_to_all | solution.py:54
  340.8 1.3 copy.8
  (7 shorter events, 0.1 us)
Async XLA Ops:
  17.4 14.1 %copy-start.2 = (s32[16]{0:T(128)S(1)}, s32[16]{0:T(128)}, u32[]{:S(2)}) copy-start(s32[16]{0:T(128)} %param.6) | copy-start | bytes 196
  17.4 74.2 %all-to-all-start = ((f32[1,128,4096]{2,0,1:T(1,128)}), f32[1,128,4096]{2,0,1:T(1,128)S(1)}, u32[]{:S(2)}, u32[]{:S(2)}) async-start(f32[1,128,4096]{2,0,1:T(1,128)} %broadcast_in_dim.16), calls=%async_computation | async-start | bytes 4194304 | tf_op jit(solution)/shard_map/all_to_all | solution.py:41
  31.5 113.2 %reduce-scatter.2.cloned.1.call-start = ((), (), s32[]{:S(2)}) async-start(), calls=%async_computation.3 | async-start | bytes 2359296 | tf_op jit(solution)/shard_map/reduce_scatter | solution.py:24
  98.5 77.8 %all-gather.5.cloned.1.call-start = ((), (), s32[]{:S(2)}) async-start(), calls=%async_computation.4 | async-start | bytes 2359296 | tf_op jit(solution)/shard_map/all_gather | solution.py:27
  144.7 123.6 %all-gather.7.cloned.1.call-start = ((), (), s32[]{:S(2)}) async-start(), calls=%async_computation.5 | async-start | bytes 5242880 | tf_op jit(solution)/shard_map/all_gather | solution.py:11
  178.4 1.3 copy-start
  270.8 1.6 copy-start.1
Sparse Core Ops, SparseCore 0:
  98.6 45.9 reduce-scatter.1
  146.8 29.4 all-gather.4
  181.3 86.9 all-gather.6
